TPU v7x, 32 devices: a whole 2x2x4 slice. The times are simulated.
32 devices in a mesh: cls: 8 (over z, y), row: 4 (over x, core).
Axes of the slice: x: 2, y: 2, z: 4, core: 2. Of those that a mesh axis runs over, the one named last changes fastest.
Arguments:
- embeddings: float32 [1024, 1024], P('row'), may hold values from -6 to 6
- weights: float32 [1024, 81920], P(('cls', 'row')), may hold values from -4 to 4
- labels: int32 [1024], replicated, may hold values from 0 to 81919, as said below
Outputs:
- weight_update: float32 [1024, 81920], P(None, ('cls', 'row'))
- losses: float32 [2, 1024], replicated
Inputs may be any that keep to these rules, and one draw needn't show every extreme that they name: labels take at most 512 distinct values, at most one in each aligned run of 160 classes; rows may share a label.
All inputs are finite; a program needn't handle non-finite values.
Results may differ from a plain program's by a relative error of at most 0.012.
The roundings to bfloat16 on the way count: a program that leaves them out, or rounds other values in their place, can miss the bound.
Values may be sent and summed in bfloat16 or wider, within the bound.
No kernel may reach another device: no remote copies, remote signals or barrier semaphores. Data moves between devices by JAX's collectives and lax.ppermute only.
A program may use at most 128 MiB of HBM per device.

v0:
```python
import jax
import jax.numpy as jnp
from jax import lax
from jax.sharding import PartitionSpec as P

STEPS = 2
learn_rate = 2.0


def shards(embeddings, weights, labels):
    peer_count = lax.axis_size(("cls", "row"))
    examples = lax.all_gather(embeddings.astype(jnp.bfloat16), "row", axis=0, tiled=True)
    row_count = examples.shape[0]
    feature_rows = weights.shape[0]
    class_count = weights.shape[1] // peer_count
    model_width = feature_rows * peer_count
    offset = lax.axis_index(("cls", "row")) * class_count
    columns = lax.broadcasted_iota(jnp.int32, (1, class_count), 1) + offset
    label_hit = columns == labels[:, None]
    pieces = weights.reshape(feature_rows, peer_count, class_count // 128, 128)
    block_weights = lax.all_to_all(pieces, ("cls", "row"), split_axis=1, concat_axis=0, tiled=True)[
        :, 0
    ]
    block_width = block_weights.shape[1] * 128
    flat_weights = block_weights.reshape(block_weights.shape[0], block_width)
    block_logits = jnp.dot(
        examples, flat_weights.astype(jnp.bfloat16), preferred_element_type=jnp.float32
    )
    first_logits = block_logits.reshape(row_count, block_weights.shape[1], 128)
    current = block_weights.reshape(model_width, class_count)
    logits = first_logits.reshape(row_count, class_count)
    starting = current
    loss_rows = []
    for step_index in range(STEPS):
        if step_index > 0:
            logits = jnp.dot(
                examples, current.astype(jnp.bfloat16), preferred_element_type=jnp.float32
            )
        local_peak = jnp.max(logits, axis=1)
        local_picked = jnp.sum(jnp.where(label_hit, logits, 0.0), axis=1)
        row_peak = lax.pmax(local_peak, ("cls", "row"))
        row_total, picked = lax.psum(
            (jnp.sum(jnp.exp(logits - row_peak[:, None]), axis=1), local_picked), ("cls", "row")
        )
        log_norm = row_peak + jnp.log(row_total)
        loss_rows.append(log_norm - picked)
        onehot = jnp.where(label_hit, 1.0, 0.0)
        residual = (jnp.exp(logits - log_norm[:, None]) - onehot).astype(jnp.bfloat16)
        gradient = (
            lax.dot_general(
                examples, residual, (((0,), (0,)), ((), ())), preferred_element_type=jnp.float32
            )
            / row_count
        )
        current = current - learn_rate * gradient
    return (current - starting, jnp.stack(loss_rows))


def solution(mesh):
    placed = (P("row", None), P(("cls", "row"), None), P())
    return jax.shard_map(
        shards,
        mesh=mesh,
        in_specs=placed,
        out_specs=(P(None, ("cls", "row")), P()),
        check_vma=False,
    )
```

profile of v0, /device:TPU:0, one launch (start us, length us, event | category | flops | bytes accessed | tf_op | source)
XLA Modules:
  0.0 578.8 jit_solution(8699041707677321800)
XLA Ops:
  7.2 9.4 %reshape.18 = f32[32,32,20,128]{3,2,1,0:T(8,128)} reshape(f32[32,81920]{1,0:T(8,128)} %param.4) | data formatting | bytes 20971520 | tf_op jit(solution)/shard_map/reshape | solution.py:20
  16.6 14.7 %copy.13 = f32[32,32,20,128]{3,0,2,1:T(8,128)} copy(f32[32,32,20,128]{3,2,1,0:T(8,128)} %reshape.18) | data formatting | bytes 20971520 | tf_op jit(solution)/shard_map/reshape | solution.py:20
  31.3 0.0 copy-start
  31.3 7.4 %all-to-all-start = ((f32[32,32,20,128]{3,0,2,1:T(8,128)}), f32[32,32,20,128]{3,0,2,1:T(8,128)}, u32[]{:S(2)}, u32[]{:S(2)}) async-start(f32[32,32,20,128]{3,0,2,1:T(8,128)} %copy.13), calls=%async_computation | async-start | bytes 20971520 | tf_op jit(solution)/shard_map/all_to_all | solution.py:21
  38.8 0.4 all-gather.2.cloned.1.call-start
  39.2 0.0 copy-done
  39.2 0.9 convert_element_type.15
  40.1 0.0 all-gather.2.cloned.1.call-update
  40.1 234.6 %all-to-all-done = f32[32,32,20,128]{3,0,2,1:T(8,128)} async-done(((f32[32,32,20,128]{3,0,2,1:T(8,128)}), f32[32,32,20,128]{3,0,2,1:T(8,128)}, u32[]{:S(2)}, u32[]{:S(2)}) %all-to-all-start) | async-done | bytes 10485792 | tf_op jit(solution)/shard_map/all_to_all | solution.py:21
  274.7 17.8 %copy.14 = f32[32,32,1,20,128]{4,3,1,0,2:T(8,128)} copy(f32[32,32,1,20,128]{4,1,3,0,2:T(8,128)} %bitcast.1) | data formatting | bytes 20971520 | tf_op jit(solution)/shard_map/all_to_all | solution.py:21
  292.5 21.9 %copy.21 = f32[128,8,20,128]{3,1,2,0:T(8,128)} copy(f32[128,8,20,128]{3,2,1,0:T(8,128)} %bitcast.41) | data formatting | bytes 20971520
  314.4 11.4 %copy.15 = f32[1024,2560]{0,1:T(8,128)} copy(f32[1024,2560]{1,0:T(8,128)} %bitcast.42) | data formatting | bytes 20971520 | tf_op jit(solution)/shard_map/reshape;squeeze | solution.py:30
  325.8 0.0 copy-start.1
  325.8 0.0 all-gather.2.cloned.1.call-done
  325.8 11.4 %fusion.35 = (f32[1024]{0:T(1024)S(1)}, f32[1024,2560]{1,0:T(8,128)}) fusion(bf16[1024,1024]{1,0:T(8,128)(2,1)} %all-gather.2.cloned.1.call-done, f32[1024,2560]{1,0:T(8,128)} %bitcast.43), kind=kOutput, calls=%fused_computation.45 | convolution fusion | flops 5373950976 | bytes 23072768 | tf_op jit(solution)/shard_map/dot_general | solution.py:26
  337.2 36.8 %pmax.14 = f32[1024]{0:T(1024)S(1)} all-reduce(f32[1024]{0:T(1024)S(1)} %get-tuple-element.17), channel_id=1, replica_groups=mesh['cls'=8,'row'=4] {'cls','row'}, use_global_device_ids=true, to_apply=%region_1.2 | all-reduce | flops 1024 | bytes 8192 | tf_op jit(solution)/shard_map/pmax | solution.py:41
  374.0 0.0 copy-done.1
  374.0 0.0 slice-start
  374.0 5.7 fusion.4
  379.7 41.0 %psum.28 = f32[1024]{0:T(1024)S(1)} all-reduce(f32[1024]{0:T(1024)S(1)} %get-tuple-element.9), channel_id=1, replica_groups=mesh['cls'=8,'row'=4] {'cls','row'}, use_global_device_ids=true, to_apply=%region_3.4 | all-reduce | flops 1024 | bytes 8192 | tf_op jit(solution)/shard_map/psum | solution.py:42
  420.7 0.0 slice-start.1
  420.7 0.0 slice-start.2
  420.7 0.0 copy-start.2
  420.7 12.0 %fusion.14 = f32[2560,1024]{1,0:T(8,128)} fusion(bf16[1024,1024]{1,0:T(8,128)(2,1)} %all-gather.2.cloned.1.call-done, f32[1024,2560]{1,0:T(8,128)} %get-tuple-element.18, s32[2560]{0:T(1024)S(1)} %iota_add_fusion, f32[1024]{0:T(1024)S(1)} %log_add_fusion.1, s32[1024]{0:T(1024)S(1)} %copy-done.1), kind=kOutput, calls=%fused_computation.21 | convolution fusion | flops 5381816320 | bytes 23087104 | tf_op jit(solution)/shard_map/dot_general | solution.py:50
  432.8 0.0 slice-done
  432.8 0.0 slice-done.1
  432.8 0.0 slice-done.2
  432.8 0.0 copy-done.2
  432.8 12.4 %fusion.36 = (f32[1024]{0:T(1024)S(1)}, f32[2560,1024]{1,0:T(8,128)}) fusion(bf16[1024,1024]{1,0:T(8,128)(2,1)S(1)} %copy-done.2, f32[1024,2560]{0,1:T(8,128)S(1)} %bitcast.45, f32[2560,1024]{1,0:T(8,128)} %fusion.14), kind=kOutput, calls=%fused_computation.46 | convolution fusion | flops 5379193856 | bytes 33558528 | tf_op jit(solution)/shard_map/dot_general | solution.py:36
  445.2 39.6 %pmax.15 = f32[1024]{0:T(1024)S(1)} all-reduce(f32[1024]{0:T(1024)S(1)} %get-tuple-element.19), channel_id=1, replica_groups=mesh['cls'=8,'row'=4] {'cls','row'}, use_global_device_ids=true, to_apply=%region_5.6 | all-reduce | flops 1024 | bytes 8192 | tf_op jit(solution)/shard_map/pmax | solution.py:41
  484.8 11.5 %copy.16 = f32[2560,1024]{0,1:T(8,128)} copy(f32[2560,1024]{1,0:T(8,128)} %get-tuple-element.20) | data formatting | bytes 20971520 | tf_op jit(solution)/shard_map/dot_general | solution.py:36
  496.3 5.6 fusion.5
  501.9 40.6 %all-reduce = (f32[1024]{0:T(1024)S(1)}, f32[1024]{0:T(1024)S(1)}, f32[1024]{0:T(1024)S(1)}) all-reduce(f32[1024]{0:T(1024)S(1)} %get-tuple-element.11, f32[1024]{0:T(1024)S(1)} %get-tuple-element.10, f32[1024]{0:T(1024)S(1)} %get-tuple-element.8), channel_id=1, replica_groups=mesh['cls'=8,'row'=4] {'cls','row'}, use_global_device_ids=true, to_apply=%region_7.8 | all-reduce | flops 3072 | bytes 24576 | tf_op jit(solution)/shard_map/psum | solution.py:42
  542.5 17.2 %fusion.6 = f32[1024,2560]{0,1:T(8,128)} fusion(f32[1024,2560]{0,1:T(8,128)} %copy.15, f32[2560,1024]{1,0:T(8,128)} %fusion.14, bf16[1024,1024]{1,0:T(8,128)(2,1)} %all-gather.2.cloned.1.call-done, f32[2560,1024]{0,1:T(8,128)} %copy.16, f32[1024]{0:T(1024)S(1)} %get-tuple-element.16, s32[2560]{0:T(1024)S(1)} %iota_add_fusion, s32[1024]{0:T(1024)S(1)} %copy-done.1), kind=kOutput, calls=%fused_computation.11 | convolution fusion | flops 5394923520 | bytes 44058624 | tf_op jit(solution)/shard_map/dot_general | solution.py:50
  559.7 11.4 %copy.18 = f32[1024,2560]{1,0:T(8,128)} copy(f32[1024,2560]{0,1:T(8,128)} %fusion.6) | data formatting | bytes 20971520
  571.1 0.6 pad_maximum_fusion
  (5 shorter events, 0.0 us)
Async XLA Ops:
  31.3 7.9 %copy-start = (f32[256,1024]{1,0:T(8,128)S(1)}, f32[256,1024]{1,0:T(8,128)}, u32[]{:S(2)}) copy-start(f32[256,1024]{1,0:T(8,128)} %param.3) | copy-start | bytes 3145732
  31.3 243.4 %all-to-all-start = ((f32[32,32,20,128]{3,0,2,1:T(8,128)}), f32[32,32,20,128]{3,0,2,1:T(8,128)}, u32[]{:S(2)}, u32[]{:S(2)}) async-start(f32[32,32,20,128]{3,0,2,1:T(8,128)} %copy.13), calls=%async_computation | async-start | bytes 20971520 | tf_op jit(solution)/shard_map/all_to_all | solution.py:21
  38.8 287.0 %all-gather.2.cloned.1.call-start = ((), (), s32[]{:S(2)}) async-start(), calls=%async_computation.1 | async-start | bytes 2621440 | tf_op jit(solution)/shard_map/all_gather | solution.py:12
  325.8 48.2 %copy-start.1 = (s32[1024]{0:T(1024)S(1)}, s32[1024]{0:T(1024)}, u32[]{:S(2)}) copy-start(s32[1024]{0:T(1024)} %param.5) | copy-start | bytes 12292
  374.0 58.8 %slice-start = ((s8[10485760]{0:T(1024)(128)(4,1)}), s8[2097152]{0:T(1024)(128)(4,1)S(1)}, s32[]{:S(2)}) async-start(s8[10485760]{0:T(1024)(128)(4,1)} %bitcast.44), calls=%async_computation.2 | async-start | bytes 4194304
  420.7 12.0 %slice-start.1 = ((s8[10485760]{0:T(1024)(128)(4,1)}), s8[4194304]{0:T(1024)(128)(4,1)S(1)}, s32[]{:S(2)}) async-start(s8[10485760]{0:T(1024)(128)(4,1)} %bitcast.44), calls=%async_computation.3 | async-start | bytes 8388608
  420.7 12.0 %slice-start.2 = ((s8[10485760]{0:T(1024)(128)(4,1)}), s8[4194304]{0:T(1024)(128)(4,1)S(1)}, s32[]{:S(2)}) async-start(s8[10485760]{0:T(1024)(128)(4,1)} %bitcast.44), calls=%async_computation.4 | async-start | bytes 8388608
  420.7 12.0 %copy-start.2 = (bf16[1024,1024]{1,0:T(8,128)(2,1)S(1)}, bf16[1024,1024]{1,0:T(8,128)(2,1)}, u32[]{:S(2)}) copy-start(bf16[1024,1024]{1,0:T(8,128)(2,1)} %all-gather.2.cloned.1.call-done) | copy-start | bytes 6291460
Sparse Core Ops, SparseCore 0:
  41.1 74.9 all-gather.1
where the time goes:
time: 585 us; the launch traced here: 579 us
  waiting for transfers between devices  235 us (40%)
  blocking collectives  158 us (27%)
  local copies, waits for them, and re-layouts  98.1 us (17%)
  matrix products  52.9 us (9%)
  between operations  14.3 us (2%)
  other arithmetic  12.8 us (2%)
  starting transfers between devices  7.86 us (1%)
    all_to_all x1, waiting for transfers between devices, shards(): lax.all_to_all(pieces, ('cls', 'row'), split_axis=1, concat_axis=0, tiled...  235 us
    psum x2, blocking collectives, shards(): lax.psum((jnp.sum(jnp.exp(logits - row_peak[:, None]), axis=1), local_pic...  81.7 us
    pmax x2, blocking collectives, shards(): row_peak = lax.pmax(local_peak, ('cls', 'row'))  76.4 us
    unnamed x14, local copies, waits for them, and re-layouts  33.3 us
    dot_general x2, matrix products, shards(): lax.dot_general(examples, residual, (((0,), (0,)), ((), ())), preferred_e...  29.2 us
    reshape x2, local copies, waits for them, and re-layouts, shards(): pieces = weights.reshape(feature_rows, peer_count, class_count // 128, 128)  24.2 us
    all_to_all x1, local copies, waits for them, and re-layouts, shards(): lax.all_to_all(pieces, ('cls', 'row'), split_axis=1, concat_axis=0, tiled...  17.8 us
    dot_general x1, matrix products, shards(): jnp.dot(examples, current.astype(jnp.bfloat16), preferred_element_type=jn...  12.4 us
  transfers between devices with their start and end apart: 2, of which 1 were waited for; matrix products, arithmetic and copies ran while one was open for 9% of the time, Pallas kernels for 0%

commit v1 on v0

--- a/solution.py
+++ b/solution.py
@@ -5,6 +5,11 @@
 
 STEPS = 2
 learn_rate = 2.0
+
+
+def axis_by_axis(value, one, other):
+    partial = lax.psum(value, one)
+    return lax.psum(partial, other)
 
 
 def shards(embeddings, weights, labels):
@@ -39,8 +44,8 @@
         local_peak = jnp.max(logits, axis=1)
         local_picked = jnp.sum(jnp.where(label_hit, logits, 0.0), axis=1)
         row_peak = lax.pmax(local_peak, ("cls", "row"))
-        row_total, picked = lax.psum(
-            (jnp.sum(jnp.exp(logits - row_peak[:, None]), axis=1), local_picked), ("cls", "row")
+        row_total, picked = axis_by_axis(
+            (jnp.sum(jnp.exp(logits - row_peak[:, None]), axis=1), local_picked), "row", "cls"
         )
         log_norm = row_peak + jnp.log(row_total)
         loss_rows.append(log_norm - picked)

time: 585 us -> 564 us (0.964)
  local copies, waits for them, and re-layouts: 98.1 us -> 87.6 us
  blocking collectives: 158 us -> 148 us
    unnamed x14, local copies, waits for them, and re-layouts: 33.3 us -> 22.7 us
    psum x2 -> x4, blocking collectives: 81.7 us -> 73.8 us  [the longest x2 57.9 us: axis_by_axis(): return lax.psum(partial, other)]
  transfers between devices with their start and end apart: 2 -> 2, of which waited for: 1 -> 1; matrix products, arithmetic and copies ran while one was open for 9% -> 7% of each run, Pallas kernels for 0% -> 0%
where the time goes in v1:
time: 564 us; the launch traced here: 558 us
  waiting for transfers between devices  234 us (41%)
  blocking collectives  148 us (26%)
  local copies, waits for them, and re-layouts  87.6 us (16%)
  matrix products  52.9 us (9%)
  between operations  14.3 us (3%)
  other arithmetic  12.8 us (2%)
  starting transfers between devices  7.95 us (1%)
    all_to_all x1, waiting for transfers between devices, shards(): lax.all_to_all(pieces, ('cls', 'row'), split_axis=1, concat_axis=0, tiled...  234 us
    pmax x2, blocking collectives, shards(): row_peak = lax.pmax(local_peak, ('cls', 'row'))  73.8 us
    psum x2, blocking collectives, axis_by_axis(): return lax.psum(partial, other)  57.9 us
    dot_general x2, matrix products, shards(): lax.dot_general(examples, residual, (((0,), (0,)), ((), ())), preferred_e...  29.2 us
    reshape x2, local copies, waits for them, and re-layouts, shards(): pieces = weights.reshape(feature_rows, peer_count, class_count // 128, 128)  24.2 us
    unnamed x14, local copies, waits for them, and re-layouts  22.7 us
    all_to_all x1, local copies, waits for them, and re-layouts, shards(): lax.all_to_all(pieces, ('cls', 'row'), split_axis=1, concat_axis=0, tiled...  17.8 us
    psum x2, blocking collectives, axis_by_axis(): partial = lax.psum(value, one)  16 us
  transfers between devices with their start and end apart: 2, of which 1 were waited for; matrix products, arithmetic and copies ran while one was open for 7% of the time, Pallas kernels for 0%

profile of v1, /device:TPU:0, one launch (start us, length us, event | category | flops | bytes accessed | tf_op | source)
XLA Modules:
  0.0 557.8 jit_solution(8873525456347711760)
XLA Ops:
  7.2 9.4 %reshape.18 = f32[32,32,20,128]{3,2,1,0:T(8,128)} reshape(f32[32,81920]{1,0:T(8,128)} %param.4) | data formatting | bytes 20971520 | tf_op jit(solution)/shard_map/reshape | solution.py:25
  16.6 14.7 %copy.13 = f32[32,32,20,128]{3,0,2,1:T(8,128)} copy(f32[32,32,20,128]{3,2,1,0:T(8,128)} %reshape.18) | data formatting | bytes 20971520 | tf_op jit(solution)/shard_map/reshape | solution.py:25
  31.3 0.0 copy-start
  31.3 7.4 %all-to-all-start = ((f32[32,32,20,128]{3,0,2,1:T(8,128)}), f32[32,32,20,128]{3,0,2,1:T(8,128)}, u32[]{:S(2)}, u32[]{:S(2)}) async-start(f32[32,32,20,128]{3,0,2,1:T(8,128)} %copy.13), calls=%async_computation | async-start | bytes 20971520 | tf_op jit(solution)/shard_map/all_to_all | solution.py:26
  38.8 0.5 all-gather.2.cloned.1.call-start
  39.3 0.0 copy-done
  39.3 0.9 convert_element_type.15
  40.2 0.0 all-gather.2.cloned.1.call-update
  40.2 234.5 %all-to-all-done = f32[32,32,20,128]{3,0,2,1:T(8,128)} async-done(((f32[32,32,20,128]{3,0,2,1:T(8,128)}), f32[32,32,20,128]{3,0,2,1:T(8,128)}, u32[]{:S(2)}, u32[]{:S(2)}) %all-to-all-start) | async-done | bytes 10485792 | tf_op jit(solution)/shard_map/all_to_all | solution.py:26
  274.7 17.8 %copy.14 = f32[32,32,1,20,128]{4,3,1,0,2:T(8,128)} copy(f32[32,32,1,20,128]{4,1,3,0,2:T(8,128)} %bitcast.1) | data formatting | bytes 20971520 | tf_op jit(solution)/shard_map/all_to_all | solution.py:26
  292.5 11.3 %copy.21 = f32[128,8,20,128]{3,1,2,0:T(8,128)} copy(f32[128,8,20,128]{3,2,1,0:T(8,128)} %bitcast.41) | data formatting | bytes 20971520
  303.9 11.4 %copy.15 = f32[1024,2560]{0,1:T(8,128)} copy(f32[1024,2560]{1,0:T(8,128)} %bitcast.42) | data formatting | bytes 20971520 | tf_op jit(solution)/shard_map/reshape;squeeze | solution.py:35
  315.2 0.0 copy-start.1
  315.2 0.0 all-gather.2.cloned.1.call-done
  315.2 11.4 %fusion.35 = (f32[1024]{0:T(1024)S(1)}, f32[1024,2560]{1,0:T(8,128)}) fusion(bf16[1024,1024]{1,0:T(8,128)(2,1)} %all-gather.2.cloned.1.call-done, f32[1024,2560]{1,0:T(8,128)} %bitcast.43), kind=kOutput, calls=%fused_computation.45 | convolution fusion | flops 5373950976 | bytes 23072768 | tf_op jit(solution)/shard_map/dot_general | solution.py:31
  326.6 36.8 %pmax.14 = f32[1024]{0:T(1024)S(1)} all-reduce(f32[1024]{0:T(1024)S(1)} %get-tuple-element.20), channel_id=1, replica_groups=mesh['cls'=8,'row'=4] {'cls','row'}, use_global_device_ids=true, to_apply=%region_1.2 | all-reduce | flops 1024 | bytes 8192 | tf_op jit(solution)/shard_map/pmax | solution.py:46
  363.4 0.0 copy-done.1
  363.4 0.0 slice-start
  363.4 5.7 %fusion.4 = (f32[1024]{0:T(1024)S(1)}, f32[1024]{0:T(1024)S(1)}) fusion(f32[1024,2560]{1,0:T(8,128)} %get-tuple-element.21, s32[2560]{0:T(1024)S(1)} %iota_add_fusion, s32[1024]{0:T(1024)S(1)} %copy-done.1, f32[1024]{0:T(1024)S(1)} %pmax.14), kind=kLoop, calls=%fused_computation.7 | loop fusion | flops 13105152 | bytes 10512384 | tf_op jit(solution)/shard_map/reduce_sum | solution.py:45
  369.2 5.8 %psum.56 = f32[1024]{0:T(1024)S(1)} all-reduce(f32[1024]{0:T(1024)S(1)} %get-tuple-element.9), channel_id=1, replica_groups=mesh['cls'=8,'row'=4] {'row'}, use_global_device_ids=true, to_apply=%region_3.4 | all-reduce | flops 1024 | bytes 8192 | tf_op jit(solution)/shard_map/psum | solution.py:11
  375.0 21.0 %psum.57 = f32[1024]{0:T(1024)S(1)} all-reduce(f32[1024]{0:T(1024)S(1)} %psum.56), channel_id=1, replica_groups=mesh['cls'=8,'row'=4] {'cls'}, use_global_device_ids=true, to_apply=%region_4.5 | all-reduce | flops 1024 | bytes 8192 | tf_op jit(solution)/shard_map/psum | solution.py:12
  396.0 0.0 slice-start.1
  396.1 0.0 slice-start.2
  396.1 0.0 copy-start.2
  396.1 12.0 %fusion.14 = f32[2560,1024]{1,0:T(8,128)} fusion(bf16[1024,1024]{1,0:T(8,128)(2,1)} %all-gather.2.cloned.1.call-done, f32[1024,2560]{1,0:T(8,128)} %get-tuple-element.21, s32[2560]{0:T(1024)S(1)} %iota_add_fusion, f32[1024]{0:T(1024)S(1)} %log_add_fusion.1, s32[1024]{0:T(1024)S(1)} %copy-done.1), kind=kOutput, calls=%fused_computation.21 | convolution fusion | flops 5381816320 | bytes 23087104 | tf_op jit(solution)/shard_map/dot_general | solution.py:55
  408.1 0.0 slice-done
  408.1 0.0 slice-done.1
  408.1 0.0 slice-done.2
  408.1 0.0 copy-done.2
  408.1 12.4 %fusion.36 = (f32[1024]{0:T(1024)S(1)}, f32[2560,1024]{1,0:T(8,128)}) fusion(bf16[1024,1024]{1,0:T(8,128)(2,1)S(1)} %copy-done.2, f32[1024,2560]{0,1:T(8,128)S(1)} %bitcast.45, f32[2560,1024]{1,0:T(8,128)} %fusion.14), kind=kOutput, calls=%fused_computation.46 | convolution fusion | flops 5379193856 | bytes 33558528 | tf_op jit(solution)/shard_map/dot_general | solution.py:41
  420.5 37.0 %pmax.15 = f32[1024]{0:T(1024)S(1)} all-reduce(f32[1024]{0:T(1024)S(1)} %get-tuple-element.22), channel_id=1, replica_groups=mesh['cls'=8,'row'=4] {'cls','row'}, use_global_device_ids=true, to_apply=%region_6.7 | all-reduce | flops 1024 | bytes 8192 | tf_op jit(solution)/shard_map/pmax | solution.py:46
  457.5 11.5 %copy.16 = f32[2560,1024]{0,1:T(8,128)} copy(f32[2560,1024]{1,0:T(8,128)} %get-tuple-element.23) | data formatting | bytes 20971520 | tf_op jit(solution)/shard_map/dot_general | solution.py:41
  469.0 5.6 %fusion.5 = (f32[1024]{0:T(1024)S(1)}, f32[1024]{0:T(1024)S(1)}) fusion(f32[2560,1024]{0,1:T(8,128)} %copy.16, s32[2560]{0:T(1024)S(1)} %iota_add_fusion, s32[1024]{0:T(1024)S(1)} %copy-done.1, f32[1024]{0:T(1024)S(1)} %pmax.15), kind=kLoop, calls=%fused_computation.8 | loop fusion | flops 13105152 | bytes 10512384 | tf_op jit(solution)/shard_map/reduce_sum | solution.py:45
  474.6 10.1 %all-reduce.1 = (f32[1024]{0:T(1024)S(1)}, f32[1024]{0:T(1024)S(1)}, f32[1024]{0:T(1024)S(1)}) all-reduce(f32[1024]{0:T(1024)S(1)} %get-tuple-element.11, f32[1024]{0:T(1024)S(1)} %get-tuple-element.10, f32[1024]{0:T(1024)S(1)} %get-tuple-element.8), channel_id=1, replica_groups=mesh['cls'=8,'row'=4] {'row'}, use_global_device_ids=true, to_apply=%region_8.9 | all-reduce | flops 3072 | bytes 24576 | tf_op jit(solution)/shard_map/psum | solution.py:11
  484.7 36.8 %all-reduce = (f32[1024]{0:T(1024)S(1)}, f32[1024]{0:T(1024)S(1)}, f32[1024]{0:T(1024)S(1)}) all-reduce(f32[1024]{0:T(1024)S(1)} %get-tuple-element.15, f32[1024]{0:T(1024)S(1)} %get-tuple-element.16, f32[1024]{0:T(1024)S(1)} %get-tuple-element.17), channel_id=1, replica_groups=mesh['cls'=8,'row'=4] {'cls'}, use_global_device_ids=true, to_apply=%region_9.10 | all-reduce | flops 3072 | bytes 24576 | tf_op jit(solution)/shard_map/psum | solution.py:12
  521.5 17.2 %fusion.6 = f32[1024,2560]{0,1:T(8,128)} fusion(f32[1024,2560]{0,1:T(8,128)} %copy.15, f32[2560,1024]{1,0:T(8,128)} %fusion.14, bf16[1024,1024]{1,0:T(8,128)(2,1)} %all-gather.2.cloned.1.call-done, f32[2560,1024]{0,1:T(8,128)} %copy.16, f32[1024]{0:T(1024)S(1)} %get-tuple-element.19, s32[2560]{0:T(1024)S(1)} %iota_add_fusion, s32[1024]{0:T(1024)S(1)} %copy-done.1), kind=kOutput, calls=%fused_computation.11 | convolution fusion | flops 5394923520 | bytes 44058624 | tf_op jit(solution)/shard_map/dot_general | solution.py:55
  538.7 11.4 %copy.18 = f32[1024,2560]{1,0:T(8,128)} copy(f32[1024,2560]{0,1:T(8,128)} %fusion.6) | data formatting | bytes 20971520
  550.1 0.6 pad_maximum_fusion
  (5 shorter events, 0.0 us)
Async XLA Ops:
  31.3 8.0 %copy-start = (f32[256,1024]{1,0:T(8,128)S(1)}, f32[256,1024]{1,0:T(8,128)}, u32[]{:S(2)}) copy-start(f32[256,1024]{1,0:T(8,128)} %param.3) | copy-start | bytes 3145732
  31.3 243.4 %all-to-all-start = ((f32[32,32,20,128]{3,0,2,1:T(8,128)}), f32[32,32,20,128]{3,0,2,1:T(8,128)}, u32[]{:S(2)}, u32[]{:S(2)}) async-start(f32[32,32,20,128]{3,0,2,1:T(8,128)} %copy.13), calls=%async_computation | async-start | bytes 20971520 | tf_op jit(solution)/shard_map/all_to_all | solution.py:26
  38.8 276.5 %all-gather.2.cloned.1.call-start = ((), (), s32[]{:S(2)}) async-start(), calls=%async_computation.1 | async-start | bytes 2621440 | tf_op jit(solution)/shard_map/all_gather | solution.py:17
  315.2 48.2 %copy-start.1 = (s32[1024]{0:T(1024)S(1)}, s32[1024]{0:T(1024)}, u32[]{:S(2)}) copy-start(s32[1024]{0:T(1024)} %param.5) | copy-start | bytes 12292
  363.4 44.7 %slice-start = ((s8[10485760]{0:T(1024)(128)(4,1)}), s8[2097152]{0:T(1024)(128)(4,1)S(1)}, s32[]{:S(2)}) async-start(s8[10485760]{0:T(1024)(128)(4,1)} %bitcast.44), calls=%async_computation.2 | async-start | bytes 4194304
  396.0 12.0 %slice-start.1 = ((s8[10485760]{0:T(1024)(128)(4,1)}), s8[4194304]{0:T(1024)(128)(4,1)S(1)}, s32[]{:S(2)}) async-start(s8[10485760]{0:T(1024)(128)(4,1)} %bitcast.44), calls=%async_computation.3 | async-start | bytes 8388608
  396.1 12.0 %slice-start.2 = ((s8[10485760]{0:T(1024)(128)(4,1)}), s8[4194304]{0:T(1024)(128)(4,1)S(1)}, s32[]{:S(2)}) async-start(s8[10485760]{0:T(1024)(128)(4,1)} %bitcast.44), calls=%async_computation.4 | async-start | bytes 8388608
  396.1 12.0 %copy-start.2 = (bf16[1024,1024]{1,0:T(8,128)(2,1)S(1)}, bf16[1024,1024]{1,0:T(8,128)(2,1)}, u32[]{:S(2)}) copy-start(bf16[1024,1024]{1,0:T(8,128)(2,1)} %all-gather.2.cloned.1.call-done) | copy-start | bytes 6291460
Sparse Core Ops, SparseCore 0:
  41.1 74.9 all-gather.1
